TPU v7x, 8 devices: a whole 2x2x1 slice. The times are simulated.
8 devices in a mesh: dp: 2 (over y, z), sp: 4 (over x, core).
Axes of the slice: x: 2, y: 2, z: 1, core: 2. Of those that a mesh axis runs over, the one named last changes fastest.
Arguments:
- q: bfloat16 [64, 24, 128], P('dp'), parts along dimension 0
- k: bfloat16 [64, 4096, 8, 128], P('dp', 'sp'), parts along dimension 0
- v: bfloat16 [64, 4096, 8, 128], P('dp', 'sp'), parts along dimension 0
Outputs:
- q: bfloat16 [64, 24, 128], P('dp'), parts along dimension 0
There are 2 independent parts. A program takes and returns all parts, laid end to end along the dimension named above; each array names one.
All inputs are finite; a program needn't handle non-finite values.
Results may differ from a plain program's by a relative error of at most 0.012.
Values are sent between devices in bfloat16 or wider.
A program may use at most 2 GiB of HBM per device.

v0:
```python
import jax
import jax.numpy as jnp
from jax import lax
from jax.sharding import PartitionSpec as P


def einsum(form, a, b):
    return jnp.einsum(form, a.astype(jnp.float32), b.astype(jnp.float32))


def part_of(q, k, v):
    grouped = q.reshape(q.shape[0], k.shape[2], -1, q.shape[2])
    scores = einsum("bgsd,bugd->bgsu", grouped, k) * q.shape[2] ** -0.5
    high = jnp.max(scores, -1, keepdims=True)
    weights = jnp.exp(scores - high)
    seen = einsum("bgsu,bugd->bgsd", weights.astype(jnp.bfloat16), v)
    return jnp.concatenate([seen, jnp.sum(weights, -1, keepdims=True), high], -1)


def together(parts):
    seen, total, high = parts[..., :-2], parts[..., -2:-1], parts[..., -1:]
    scale = jnp.exp(high - jnp.max(high, 0))
    return (jnp.sum(seen * scale, 0) / jnp.sum(total * scale, 0)).astype(jnp.bfloat16)


def solution(mesh):
    def step(q, k, v):
        return together(lax.all_gather(part_of(q, k, v), "sp")).reshape(q.shape)

    return jax.shard_map(
        step,
        mesh=mesh,
        in_specs=(P("dp", None, None), P("dp", "sp", None, None), P("dp", "sp", None, None)),
        out_specs=P("dp", None, None),
        check_vma=False,
    )
```

profile of v0, /device:TPU:0, one launch (start us, length us, event | category | flops | bytes accessed | tf_op | source)
XLA Modules:
  0.0 114.6 jit_solution(13958155971949872325)
XLA Ops:
  6.5 0.0 all-gather.3.cloned.1.call-start
  6.5 1.0 copy.46
  7.5 26.1 %multiply_reduce_fusion = (f32[32,8,3]{2,1,0:T(8,128)S(1)}, f32[32,8,3,1024]{3,2,1,0:T(4,128)S(1)}) fusion(bf16[32,1024,8,128]{3,2,1,0:T(8,128)(2,1)} %param.4, bf16[32,8,3,128]{3,0,2,1:T(8,128)(2,1)S(1)} %bitcast.15), kind=kOutput, calls=%fused_computation.5 | convolution fusion | flops 202898688 | bytes 70454272 | tf_op jit(solution)/shard_map/bgsd,bugd->bgsu/dot_general | solution.py:8
  33.6 0.0 copy-start
  33.6 1.9 %copy-done = f32[32,8,3,1024]{3,2,1,0:T(4,128)} copy-done((f32[32,8,3,1024]{3,2,1,0:T(4,128)}, f32[32,8,3,1024]{3,2,1,0:T(4,128)S(1)}, u32[]{:S(2)}) %copy-start) | copy-done | bytes 3145752
  35.6 2.1 %fusion.4 = f32[32,8,3]{2,1,0:T(8,128)S(1)} fusion(f32[32,8,3,1024]{3,2,1,0:T(4,128)S(1)} %get-tuple-element.11, f32[32,8,3]{2,1,0:T(8,128)S(1)} %get-tuple-element.10), kind=kLoop, calls=%fused_computation.6 | loop fusion | flops 2358528 | bytes 3151872 | tf_op jit(solution)/shard_map/reduce_sum | solution.py:17
  37.7 26.7 %fusion = f32[32,8,3,128]{3,2,1,0:T(4,128)S(1)} fusion(bf16[32,1024,8,128]{3,2,1,0:T(8,128)(2,1)} %param.5, f32[32,8,3,1024]{3,2,1,0:T(4,128)} %copy-done, f32[32,8,3]{2,1,0:T(8,128)S(1)} %get-tuple-element.10), kind=kOutput, calls=%fused_computation | convolution fusion | flops 203685888 | bytes 70650880 | tf_op jit(solution)/shard_map/bgsu,bugd->bgsd/dot_general | solution.py:8
  64.4 1.7 %copy.52 = f32[32,8,3,1]{3,2,1,0:T(4,128)S(1)} copy(f32[32,8,3,1]{2,1,0,3:T(8,128)S(1)} %bitcast.16) | data formatting | bytes 6144 | tf_op jit(solution)/shard_map/broadcast_in_dim | solution.py:17
  66.0 1.7 %copy.53 = f32[32,8,3,1]{3,2,1,0:T(4,128)S(1)} copy(f32[32,8,3,1]{2,1,0,3:T(8,128)S(1)} %bitcast.14) | data formatting | bytes 6144 | tf_op jit(solution)/shard_map/broadcast_in_dim | solution.py:14
  67.7 0.4 pad_maximum_fusion
  68.1 1.0 copy.54
  69.2 0.0 all-gather.3.cloned.1.call-update
  69.2 28.4 %all-gather.3.cloned.1.call-done = f32[128,8,3,130]{3,1,2,0:T(8,128)} async-done(((f32[32,8,3,130]{3,1,2,0:T(8,128)}), f32[128,8,3,130]{3,1,2,0:T(8,128)}) %all-gather.3.cloned.1.call-update) | async-done | bytes 1597456 | tf_op jit(solution)/shard_map/all_gather | solution.py:28
  97.6 0.0 copy-start.1
  97.6 4.2 %fusion.14 = (f32[4,32,8,3,1]{4,2,3,1,0:T(8,128)}, f32[32,8,3]{1,2,0:T(4,128)S(1)}, f32[4,32,8,3,1]{4,2,3,1,0:T(8,128)}) fusion(f32[4,32,8,3,130]{4,2,3,1,0:T(8,128)} %bitcast.12), kind=kLoop, calls=%fused_computation.21 | loop fusion | flops 2304 | bytes 52224 | tf_op jit(solution)/shard_map/slice | solution.py:21
  101.8 2.0 %copy.68 = f32[4,32,8,3,1]{1,2,4,3,0:T(8,128)S(1)} copy(f32[4,32,8,3,1]{4,2,3,1,0:T(8,128)} %get-tuple-element.5) | data formatting | bytes 24576
  103.9 0.1 copy.70
  104.0 2.0 %copy.67 = f32[4,32,8,3,1]{1,2,4,3,0:T(8,128)S(1)} copy(f32[4,32,8,3,1]{4,2,3,1,0:T(8,128)} %get-tuple-element.7) | data formatting | bytes 24576
  106.1 0.1 copy.56
  106.2 0.0 copy-done.1
  106.2 0.5 fusion.9
  106.7 0.1 copy.58
  106.8 0.2 fusion.10
  107.0 0.8 copy.61
  (3 shorter events, 0.0 us)
Async XLA Ops:
  6.5 91.1 %all-gather.3.cloned.1.call-start = ((), (), s32[]{:S(2)}) async-start(), calls=%async_computation | async-start | bytes 3932160 | tf_op jit(solution)/shard_map/all_gather | solution.py:28
  33.6 1.9 %copy-start = (f32[32,8,3,1024]{3,2,1,0:T(4,128)}, f32[32,8,3,1024]{3,2,1,0:T(4,128)S(1)}, u32[]{:S(2)}) copy-start(f32[32,8,3,1024]{3,2,1,0:T(4,128)S(1)} %get-tuple-element.11) | copy-start | bytes 9437188
  97.6 8.6 %copy-start.1 = (f32[128,8,3,130]{3,1,2,0:T(8,128)S(1)}, f32[128,8,3,130]{3,1,2,0:T(8,128)}, u32[]{:S(2)}) copy-start(f32[128,8,3,130]{3,1,2,0:T(8,128)} %all-gather.3.cloned.1.call-done) | copy-start | bytes 4792324
Sparse Core Ops, SparseCore 0:
  69.3 28.2 all-gather.2
where the time goes:
time: 115 us
  matrix products  52.8 us (46%)
  waiting for transfers between devices  28.5 us (25%)
  between operations  13.5 us (12%)
  local copies, waits for them, and re-layouts  12.4 us (11%)
  other arithmetic  7.39 us (6%)
    dot_general x2, matrix products, einsum(): return jnp.einsum(form, a.astype(jnp.float32), b.astype(jnp.float32))  52.8 us
    all_gather x1, waiting for transfers between devices, step(): return together(lax.all_gather(part_of(q, k, v), 'sp')).reshape(q.shape)  28.4 us
    unnamed x8, local copies, waits for them, and re-layouts  7.06 us
    slice x1, other arithmetic, together(): seen, total, high = (parts[..., :-2], parts[..., -2:-1], parts[..., -1:])  4.22 us
  transfers between devices with their start and end apart: 1, of which 1 were waited for; matrix products, arithmetic and copies ran while one was open for 0% of the time, Pallas kernels for 0%

commit v1 on v0

v1 whole, which is shorter than its diff:
```python
import functools
import math

import jax
import jax.numpy as jnp
from jax import lax
from jax.experimental import pallas as pl
from jax.experimental.pallas import tpu as pltpu
from jax.sharding import PartitionSpec as P

KEYS = 6
VALUES = 6
LAG = 2
CHUNKS = 4
MESH = pl.DeviceIdType.MESH


def kernel(n, groups, q_hbm, k_hbm, v_hbm, o_hbm, q_ref, kb, vb, s0, s1, p0, p1, m0, m1, stats, parts, out, q_sem, k_sem, v_sem, last_sem, o_sem, send, recv, stat_send, stat_recv):
    heads, head = q_ref.shape[1:]
    rows = kb.shape[1]
    half = rows // 2
    tiles = half // 128
    key_heads = groups[0]
    scale = head**-0.5 * math.log2(math.e)
    me = lax.axis_index("sp")
    size = parts.shape[0]
    s_bufs, p_bufs, m_bufs = (s0, s1), (p0, p1), (m0, m1)
    lane = lax.broadcasted_iota(jnp.int32, (heads, 128), 1)

    def peer(d):
        return {"sp": lax.rem(me + d, size)}

    def source(d):
        return lax.rem(me + size - d, size)

    def k_copy(i):
        slot = lax.rem(i, KEYS)
        return pltpu.make_async_copy(k_hbm.at[i], kb.at[slot], k_sem.at[slot])

    def v_copy(i):
        slot = lax.rem(i, VALUES)
        return pltpu.make_async_copy(v_hbm.at[i], vb.at[slot], v_sem.at[slot])

    def last_copy(c):
        slot, step = (n - 1) % VALUES, half // CHUNKS
        return [
            pltpu.make_async_copy(v_hbm.at[n - 1, pl.ds(h * half + c * step, step)], vb.at[slot, pl.ds(h * half + c * step, step)], last_sem.at[h, c])
            for h in range(2)
        ]

    def part_copy(d, first, count, late, slot):
        ref = parts.at[slot, pl.ds(first, count)]
        return pltpu.make_async_remote_copy(ref, ref, send.at[d - 1], recv.at[d - 1, late], device_id=peer(d), device_id_type=MESH)

    def stat_copy(d, slot):
        return pltpu.make_async_remote_copy(stats.at[slot], stats.at[slot], stat_send.at[d - 1], stat_recv.at[d - 1], device_id=peer(d), device_id_type=MESH)

    def scores(i, u):
        q = q_ref[i]
        none = jnp.zeros_like(q)
        both = jnp.concatenate([jnp.concatenate([q, none], 1), jnp.concatenate([none, q], 1)], 0)
        slot = lax.rem(i, KEYS)
        keys = jnp.concatenate([kb[slot, :half], kb[slot, half:]], 1)
        s = lax.dot_general(both, keys, (((1,), (1,)), ((), ())), preferred_element_type=jnp.float32)
        s = jnp.where(jnp.tile(own, (1, tiles)), s, -jnp.inf)
        s_bufs[u][...] = s
        high = functools.reduce(jnp.maximum, [s[:, j * 128 : (j + 1) * 128] for j in range(tiles)])
        m_bufs[u][...] = jnp.maximum(high[:heads], high[heads:])

    def weights(i, u):
        high = jnp.max(m_bufs[u][...], 1, keepdims=True)
        w = jnp.exp2((s_bufs[u][...] - jnp.concatenate([high, high], 0)) * scale)
        p_bufs[u][lax.rem(lax.div(i, 2), LAG // 2)] = w.astype(jnp.bfloat16)
        total = functools.reduce(jnp.add, [w[:, j * 128 : (j + 1) * 128] for j in range(tiles)])
        total = jnp.sum(total[:heads] + total[heads:], 1, keepdims=True)
        stats[me, 0] = jnp.where(lane == i, high, stats[me, 0])
        stats[me, 1] = jnp.where(lane == i, total, stats[me, 1])

    def seen(i, u, begin, end, cuts):
        slot = lax.rem(i, VALUES)
        w = p_bufs[u].at[lax.rem(lax.div(i, 2), LAG // 2)]
        step = (end - begin) // cuts
        o = None
        for c in range(cuts):
            b = begin + c * step
            values = jnp.concatenate([vb[slot, b : b + step], vb[slot, half + b : half + b + step]], 1)
            x = jnp.dot(w[:, b : b + step], values, preferred_element_type=jnp.float32)
            o = x if o is None else o + x
        return o[:heads, :head] + o[heads:, head:]

    def keep(i, o):
        parts[me, i] = o.astype(jnp.bfloat16)

    def share(first, count, late):
        for d in range(1, size):
            part_copy(d, first, count, late, me).start()

    q_copy = pltpu.make_async_copy(q_hbm, q_ref, q_sem)
    q_copy.start()
    for t in range(max(KEYS, VALUES + LAG)):
        if t < KEYS:
            k_copy(t).start(priority=1)
        if 0 <= t - LAG < VALUES:
            v_copy(t - LAG).start(priority=1)
    barrier = pltpu.get_barrier_semaphore()
    for d in range(1, size):
        pl.semaphore_signal(barrier, inc=1, device_id=peer(d), device_id_type=MESH)
    row = lax.broadcasted_iota(jnp.int32, (2 * heads, 128), 0)
    col = lax.broadcasted_iota(jnp.int32, (2 * heads, 128), 1)
    own = lax.rem(col, key_heads) == lax.div(lax.rem(row, heads), heads // key_heads)
    stats[me] = jnp.ones_like(stats[me])
    q_copy.wait()

    k_copy(0).wait()
    scores(0, 0)
    k_copy(1).wait()
    scores(1, 1)
    weights(0, 0)
    k_copy(KEYS).start(priority=1)
    k_copy(KEYS + 1).start(priority=1)

    def start_last():
        for c in range(CHUNKS):
            for copy in last_copy(c):
                copy.start(priority=1)

    def early(j, carry):
        for u in range(2):
            k_copy(2 * j + u).wait()
        for u in range(2):
            scores(2 * j + u, u)
            weights(2 * j + u - 1, 1 - u)
        for u in range(2):
            k_copy(2 * j + u + KEYS).start(priority=1)
        return carry

    lax.fori_loop(1, LAG // 2, early, 0)
    pl.semaphore_wait(barrier, size - 1)

    def step(j, carry):
        for u in range(2):
            k_copy(2 * j + u).wait()
            v_copy(2 * j + u - LAG).wait()
        for u in range(2):
            t = 2 * j + u
            keep(t - LAG, seen(t - LAG, u, 0, half, 2))
            scores(t, u)
            weights(t - 1, 1 - u)
        share(2 * j - LAG, 2, 0)
        for u in range(2):
            t = 2 * j + u

            @pl.when(t + KEYS < n)
            def _():
                k_copy(t + KEYS).start(priority=1)

            @pl.when(t - LAG + VALUES < n - 1)
            def _():
                v_copy(t - LAG + VALUES).start(priority=1)

            @pl.when(t - LAG + VALUES == n - 1)
            def _():
                start_last()

        return carry

    lax.fori_loop(LAG // 2, n // 2, step, 0)
    weights(n - 1, 1)
    for d in range(1, size):
        stat_copy(d, me).start()

    def late(j, carry):
        for u in range(2):
            i = 2 * j + u
            v_copy(i).wait()
            keep(i, seen(i, u, 0, half, 2))
        share(2 * j, 2, 0)
        return carry

    lax.fori_loop((n - LAG) // 2, n // 2 - 1, late, 0)
    v_copy(n - 2).wait()
    keep(n - 2, seen(n - 2, 0, 0, half, 2))
    share(n - 2, 1, 1)
    o = None
    for c in range(CHUNKS):
        for copy in last_copy(c):
            copy.wait()
        x = seen(n - 1, 1, c * (half // CHUNKS), (c + 1) * (half // CHUNKS), 2)
        o = x if o is None else o + x
    keep(n - 1, o)
    share(n - 1, 1, 1)

    for d in range(1, size):
        stat_copy(d, source(d)).wait_recv()
    highs = [stats[r, 0] for r in range(size)]
    high = functools.reduce(jnp.maximum, highs)
    factors = [jnp.exp2((h - high) * scale) for h in highs]
    total = functools.reduce(jnp.add, [f * stats[r, 1] for r, f in enumerate(factors)])
    factors = [f / total for f in factors]

    def together(i):
        terms = [parts[r, i].astype(jnp.float32) * f[:, i : i + 1] for r, f in enumerate(factors)]
        out[i] = functools.reduce(jnp.add, terms).astype(out.dtype)

    for d in range(1, size):
        part_copy(d, 0, n - 2, 0, source(d)).wait_recv()
    for i in range(n - 2):
        together(i)
    most = pltpu.make_async_copy(out.at[pl.ds(0, n - 2)], o_hbm.at[pl.ds(0, n - 2)], o_sem.at[0])
    most.start()
    for d in range(1, size):
        part_copy(d, n - 2, 2, 1, source(d)).wait_recv()
    for x in range(2):
        together(n - 2 + x)
    rest = pltpu.make_async_copy(out.at[pl.ds(n - 2, 2)], o_hbm.at[pl.ds(n - 2, 2)], o_sem.at[1])
    rest.start()
    for d in range(1, size):
        stat_copy(d, me).wait_send()
        part_copy(d, 0, n, 0, me).wait_send()
    most.wait()
    rest.wait()


def solution(mesh):
    size = mesh.shape["sp"]

    def step(q, k, v):
        n, heads, head = q.shape
        tokens, key_heads = k.shape[1:3]
        rows = tokens * key_heads
        half = rows // 2
        f32 = jnp.float32
        dma = pltpu.SemaphoreType.DMA
        return pl.pallas_call(
            functools.partial(kernel, n, (key_heads,)),
            out_shape=jax.ShapeDtypeStruct(q.shape, q.dtype),
            in_specs=[pl.BlockSpec(memory_space=pl.ANY)] * 3,
            out_specs=pl.BlockSpec(memory_space=pl.ANY),
            scratch_shapes=[
                pltpu.VMEM(q.shape, q.dtype),
                pltpu.VMEM((KEYS, rows, head), k.dtype),
                pltpu.VMEM((VALUES, rows, head), v.dtype),
                *[pltpu.VMEM((2 * heads, half), f32)] * 2,
                *[pltpu.VMEM((LAG // 2, 2 * heads, half), jnp.bfloat16)] * 2,
                *[pltpu.VMEM((heads, 128), f32)] * 2,
                pltpu.VMEM((size, 2, heads, 128), f32),
                pltpu.VMEM((size, n, heads, head), jnp.bfloat16),
                pltpu.VMEM(q.shape, q.dtype),
                dma,
                dma((KEYS,)),
                dma((VALUES,)),
                dma((2, CHUNKS)),
                dma((2,)),
                dma((size - 1,)),
                dma((size - 1, 2)),
                dma((size - 1,)),
                dma((size - 1,)),
            ],
            compiler_params=pltpu.CompilerParams(collective_id=0, has_side_effects=True, vmem_limit_bytes=60 * 2**20),
            name="attend",
        )(q, k.reshape(n, rows, head), v.reshape(n, rows, head))

    return jax.shard_map(
        step,
        mesh=mesh,
        in_specs=(P("dp", None, None), P("dp", "sp", None, None), P("dp", "sp", None, None)),
        out_specs=P("dp", None, None),
        check_vma=False,
    )
```

time: 115 us -> 50.4 us (0.44)
  matrix products: 52.8 us -> 0 us
  Pallas kernels: 0 us -> 48.7 us
  waiting for transfers between devices: 28.5 us -> 0 us
  between operations: 13.5 us -> 0.01 us
  local copies, waits for them, and re-layouts: 12.4 us -> 1.62 us
  other arithmetic: 7.39 us -> 0 us
    dot_general x2 -> x0, matrix products: 52.8 us -> none  [einsum(): return jnp.einsum(form, a.astype(jnp.float32), b.astype(jnp.float32))]
    pallas_call x0 -> x1, Pallas kernels: none -> 48.7 us  [step(): pl.pallas_call(functools.partial(kernel, n, (key_heads,)), out_shape=jax....]
    all_gather x1 -> x0, waiting for transfers between devices: 28.4 us -> none  [step(): return together(lax.all_gather(part_of(q, k, v), 'sp')).reshape(q.shape)]
    unnamed x8 -> x1, local copies, waits for them, and re-layouts: 7.06 us -> 1.62 us
    slice x1 -> x0, other arithmetic: 4.22 us -> none  [together(): seen, total, high = (parts[..., :-2], parts[..., -2:-1], parts[..., -1:])]
    broadcast_in_dim x2 -> x0, local copies, waits for them, and re-layouts: 3.33 us -> none  [the longest x1 1.66 us: part_of(): jnp.sum(weights, -1, keepdims=True)]
    reduce_sum x3 -> x0, other arithmetic: 2.58 us -> none  [the longest x1 2.09 us: part_of(): jnp.sum(weights, -1, keepdims=True)]
  transfers between devices with their start and end apart: 1 -> 0, of which waited for: 1 -> 0; matrix products, arithmetic and copies ran while one was open for 0% -> 0% of each run, Pallas kernels for 0% -> 0%
where the time goes in v1:
time: 50.4 us; the launch traced here: 50.3 us
  Pallas kernels  48.7 us (97%)
  local copies, waits for them, and re-layouts  1.62 us (3%)
    pallas_call x1, Pallas kernels, step(): pl.pallas_call(functools.partial(kernel, n, (key_heads,)), out_shape=jax....  48.7 us
    unnamed x1, local copies, waits for them, and re-layouts  1.62 us

profile of v1, /device:TPU:0, one launch (start us, length us, event | category | flops | bytes accessed | tf_op | source)
XLA Modules:
  0.0 50.3 jit_solution(8495871607237243657)
XLA Ops:
  0.0 48.7 %attend.1 = bf16[32,24,128]{2,1,0:T(8,128)(2,1)} custom-call(bf16[32,24,128]{2,1,0:T(8,128)(2,1)} %q_hbm.1, bf16[32,8192,128]{2,1,0:T(8,128)(2,1)} %bitcast.k_hbm, bf16[32,8192,128]{2,1,0:T(8,128)(2,1)} %bitcast.1.v_hbm), custom_call_target="tpu_custom_call" | custom-call | tf_op jit(solution)/shard_map/attend/pallas_call | solution.py:234
  48.7 1.6 %copy.5 = bf16[32,24,128]{2,1,0:T(8,128)(2,1)} copy(bf16[32,24,128]{2,1,0:T(8,128)(2,1)} %attend.1) | data formatting | bytes 393216

commit v2 on v1

--- a/solution.py
+++ b/solution.py
@@ -8,18 +8,19 @@
 from jax.experimental.pallas import tpu as pltpu
 from jax.sharding import PartitionSpec as P
 
-KEYS = 6
-VALUES = 6
-LAG = 2
-CHUNKS = 4
+KEYS = 8
+VALUES = 8
+LAG = 12
+CUTS = (1 / 2,)
 MESH = pl.DeviceIdType.MESH
 
 
-def kernel(n, groups, q_hbm, k_hbm, v_hbm, o_hbm, q_ref, kb, vb, s0, s1, p0, p1, m0, m1, stats, parts, out, q_sem, k_sem, v_sem, last_sem, o_sem, send, recv, stat_send, stat_recv):
+def kernel(n, groups, q_hbm, k_hbm, v_hbm, out, q_ref, kb, vb, s0, s1, p0, p1, m0, m1, stats, parts, q_sem, k_sem, v_sem, last_sem, send, recv, stat_send, stat_recv):
     heads, head = q_ref.shape[1:]
     rows = kb.shape[1]
     half = rows // 2
     tiles = half // 128
+    ends = [0, *(int(c * rows) for c in CUTS), rows]
     key_heads = groups[0]
     scale = head**-0.5 * math.log2(math.e)
     me = lax.axis_index("sp")
@@ -42,11 +43,8 @@
         return pltpu.make_async_copy(v_hbm.at[i], vb.at[slot], v_sem.at[slot])
 
     def last_copy(c):
-        slot, step = (n - 1) % VALUES, half // CHUNKS
-        return [
-            pltpu.make_async_copy(v_hbm.at[n - 1, pl.ds(h * half + c * step, step)], vb.at[slot, pl.ds(h * half + c * step, step)], last_sem.at[h, c])
-            for h in range(2)
-        ]
+        slot, run = (n - 1) % VALUES, pl.ds(ends[c], ends[c + 1] - ends[c])
+        return pltpu.make_async_copy(v_hbm.at[n - 1, run], vb.at[slot, run], last_sem.at[c])
 
     def part_copy(d, first, count, late, slot):
         ref = parts.at[slot, pl.ds(first, count)]
@@ -76,32 +74,26 @@
         stats[me, 0] = jnp.where(lane == i, high, stats[me, 0])
         stats[me, 1] = jnp.where(lane == i, total, stats[me, 1])
 
-    def seen(i, u, begin, end, cuts):
-        slot = lax.rem(i, VALUES)
+    def seen(i, u, begin, end):
+        slot, h = lax.rem(i, VALUES), begin // half
         w = p_bufs[u].at[lax.rem(lax.div(i, 2), LAG // 2)]
-        step = (end - begin) // cuts
-        o = None
-        for c in range(cuts):
-            b = begin + c * step
-            values = jnp.concatenate([vb[slot, b : b + step], vb[slot, half + b : half + b + step]], 1)
-            x = jnp.dot(w[:, b : b + step], values, preferred_element_type=jnp.float32)
-            o = x if o is None else o + x
-        return o[:heads, :head] + o[heads:, head:]
+        w = w[h * heads : (h + 1) * heads, begin - h * half : end - h * half]
+        return jnp.dot(w, vb[slot, begin:end], preferred_element_type=jnp.float32)
+
+    def seen_all(i, u):
+        return seen(i, u, 0, half) + seen(i, u, half, rows)
 
     def keep(i, o):
         parts[me, i] = o.astype(jnp.bfloat16)
 
     def share(first, count, late):
-        for d in range(1, size):
+        for d in sorted(range(1, size), key=lambda d: abs(2 * d - size)):
             part_copy(d, first, count, late, me).start()
 
     q_copy = pltpu.make_async_copy(q_hbm, q_ref, q_sem)
     q_copy.start()
-    for t in range(max(KEYS, VALUES + LAG)):
-        if t < KEYS:
-            k_copy(t).start(priority=1)
-        if 0 <= t - LAG < VALUES:
-            v_copy(t - LAG).start(priority=1)
+    for i in range(KEYS):
+        k_copy(i).start(priority=1)
     barrier = pltpu.get_barrier_semaphore()
     for d in range(1, size):
         pl.semaphore_signal(barrier, inc=1, device_id=peer(d), device_id_type=MESH)
@@ -116,15 +108,25 @@
     k_copy(1).wait()
     scores(1, 1)
     weights(0, 0)
-    k_copy(KEYS).start(priority=1)
-    k_copy(KEYS + 1).start(priority=1)
+    for i in range(2):
+        k_copy(KEYS + i).start(priority=1)
+    for i in range(VALUES - LAG + 2):
+        v_copy(i).start(priority=1)
 
     def start_last():
-        for c in range(CHUNKS):
-            for copy in last_copy(c):
-                copy.start(priority=1)
-
-    def early(j, carry):
+        for c in range(len(CUTS) + 1):
+            last_copy(c).start(priority=1)
+
+    def next_values(i):
+        @pl.when(i < n - 1)
+        def _():
+            v_copy(i).start(priority=1)
+
+        @pl.when(i == n - 1)
+        def _():
+            start_last()
+
+    def early(values, j, carry):
         for u in range(2):
             k_copy(2 * j + u).wait()
         for u in range(2):
@@ -132,9 +134,13 @@
             weights(2 * j + u - 1, 1 - u)
         for u in range(2):
             k_copy(2 * j + u + KEYS).start(priority=1)
+            if values:
+                v_copy(2 * j + u - LAG + VALUES).start(priority=1)
         return carry
 
-    lax.fori_loop(1, LAG // 2, early, 0)
+    first = max(1, (LAG - VALUES) // 2)
+    lax.fori_loop(1, first, functools.partial(early, False), 0)
+    lax.fori_loop(first, LAG // 2, functools.partial(early, True), 0)
     pl.semaphore_wait(barrier, size - 1)
 
     def step(j, carry):
@@ -143,7 +149,7 @@
             v_copy(2 * j + u - LAG).wait()
         for u in range(2):
             t = 2 * j + u
-            keep(t - LAG, seen(t - LAG, u, 0, half, 2))
+            keep(t - LAG, seen_all(t - LAG, u))
             scores(t, u)
             weights(t - 1, 1 - u)
         share(2 * j - LAG, 2, 0)
@@ -154,13 +160,7 @@
             def _():
                 k_copy(t + KEYS).start(priority=1)
 
-            @pl.when(t - LAG + VALUES < n - 1)
-            def _():
-                v_copy(t - LAG + VALUES).start(priority=1)
-
-            @pl.when(t - LAG + VALUES == n - 1)
-            def _():
-                start_last()
+            next_values(t - LAG + VALUES)
 
         return carry
 
@@ -173,19 +173,20 @@
         for u in range(2):
             i = 2 * j + u
             v_copy(i).wait()
-            keep(i, seen(i, u, 0, half, 2))
+            keep(i, seen_all(i, u))
         share(2 * j, 2, 0)
+        for u in range(2):
+            next_values(2 * j + u + VALUES)
         return carry
 
     lax.fori_loop((n - LAG) // 2, n // 2 - 1, late, 0)
     v_copy(n - 2).wait()
-    keep(n - 2, seen(n - 2, 0, 0, half, 2))
+    keep(n - 2, seen_all(n - 2, 0))
     share(n - 2, 1, 1)
     o = None
-    for c in range(CHUNKS):
-        for copy in last_copy(c):
-            copy.wait()
-        x = seen(n - 1, 1, c * (half // CHUNKS), (c + 1) * (half // CHUNKS), 2)
+    for c in range(len(CUTS) + 1):
+        last_copy(c).wait()
+        x = seen(n - 1, 1, ends[c], ends[c + 1])
         o = x if o is None else o + x
     keep(n - 1, o)
     share(n - 1, 1, 1)
@@ -206,19 +207,13 @@
         part_copy(d, 0, n - 2, 0, source(d)).wait_recv()
     for i in range(n - 2):
         together(i)
-    most = pltpu.make_async_copy(out.at[pl.ds(0, n - 2)], o_hbm.at[pl.ds(0, n - 2)], o_sem.at[0])
-    most.start()
     for d in range(1, size):
         part_copy(d, n - 2, 2, 1, source(d)).wait_recv()
     for x in range(2):
         together(n - 2 + x)
-    rest = pltpu.make_async_copy(out.at[pl.ds(n - 2, 2)], o_hbm.at[pl.ds(n - 2, 2)], o_sem.at[1])
-    rest.start()
     for d in range(1, size):
         stat_copy(d, me).wait_send()
         part_copy(d, 0, n, 0, me).wait_send()
-    most.wait()
-    rest.wait()
 
 
 def solution(mesh):
@@ -233,9 +228,9 @@
         dma = pltpu.SemaphoreType.DMA
         return pl.pallas_call(
             functools.partial(kernel, n, (key_heads,)),
-            out_shape=jax.ShapeDtypeStruct(q.shape, q.dtype),
+            out_shape=pltpu.VMEM(q.shape, q.dtype),
             in_specs=[pl.BlockSpec(memory_space=pl.ANY)] * 3,
-            out_specs=pl.BlockSpec(memory_space=pl.ANY),
+            out_specs=pl.BlockSpec(memory_space=pltpu.VMEM),
             scratch_shapes=[
                 pltpu.VMEM(q.shape, q.dtype),
                 pltpu.VMEM((KEYS, rows, head), k.dtype),
@@ -245,12 +240,10 @@
                 *[pltpu.VMEM((heads, 128), f32)] * 2,
                 pltpu.VMEM((size, 2, heads, 128), f32),
                 pltpu.VMEM((size, n, heads, head), jnp.bfloat16),
-                pltpu.VMEM(q.shape, q.dtype),
                 dma,
                 dma((KEYS,)),
                 dma((VALUES,)),
-                dma((2, CHUNKS)),
-                dma((2,)),
+                dma((len(CUTS) + 1,)),
                 dma((size - 1,)),
                 dma((size - 1, 2)),
                 dma((size - 1,)),

time: 50.4 us -> 46.3 us (0.919)
  Pallas kernels: 48.7 us -> 45.5 us
  local copies, waits for them, and re-layouts: 1.62 us -> 0.68 us
    pallas_call x1, Pallas kernels: 48.7 us -> 45.5 us  [step(): pl.pallas_call(functools.partial(kernel, n, (key_heads,)), out_shape=pltp...]
    unnamed x1, local copies, waits for them, and re-layouts: 1.62 us -> 0.68 us
where the time goes in v2:
time: 46.3 us; the launch traced here: 46.2 us
  Pallas kernels  45.5 us (98%)
  local copies, waits for them, and re-layouts  0.68 us (1%)
    pallas_call x1, Pallas kernels, step(): pl.pallas_call(functools.partial(kernel, n, (key_heads,)), out_shape=pltp...  45.5 us

profile of v2, /device:TPU:0, one launch (start us, length us, event | category | flops | bytes accessed | tf_op | source)
XLA Modules:
  0.0 46.2 jit_solution(17373088543354089224)
XLA Ops:
  0.0 45.5 %attend.1 = bf16[32,24,128]{2,1,0:T(8,128)(2,1)S(1)} custom-call(bf16[32,24,128]{2,1,0:T(8,128)(2,1)} %q_hbm.1, bf16[32,8192,128]{2,1,0:T(8,128)(2,1)} %bitcast.k_hbm, bf16[32,8192,128]{2,1,0:T(8,128)(2,1)} %bitcast.1.v_hbm), custom_call_target="tpu_custom_call" | custom-call | tf_op jit(solution)/shard_map/attend/pallas_call | solution.py:229
  45.5 0.7 %copy.5 = bf16[32,24,128]{2,1,0:T(8,128)(2,1)} copy(bf16[32,24,128]{2,1,0:T(8,128)(2,1)S(1)} %attend.1) | data formatting | bytes 393216

commit v3 on v2

--- a/solution.py
+++ b/solution.py
@@ -10,18 +10,15 @@
 
 KEYS = 8
 VALUES = 8
-LAG = 12
-CUTS = (1 / 2,)
+LAG = 14
 MESH = pl.DeviceIdType.MESH
 
 
-def kernel(n, groups, q_hbm, k_hbm, v_hbm, out, q_ref, kb, vb, s0, s1, p0, p1, m0, m1, stats, parts, q_sem, k_sem, v_sem, last_sem, send, recv, stat_send, stat_recv):
+def kernel(n, key_heads, q_hbm, k_hbm, v_hbm, out, q_ref, kb, vb, s0, s1, p0, p1, m0, m1, stats, parts, recv, stat_recv, q_sem, k_sem, v_sem, send, stat_send):
     heads, head = q_ref.shape[1:]
     rows = kb.shape[1]
     half = rows // 2
     tiles = half // 128
-    ends = [0, *(int(c * rows) for c in CUTS), rows]
-    key_heads = groups[0]
     scale = head**-0.5 * math.log2(math.e)
     me = lax.axis_index("sp")
     size = parts.shape[0]
@@ -38,13 +35,9 @@
         slot = lax.rem(i, KEYS)
         return pltpu.make_async_copy(k_hbm.at[i], kb.at[slot], k_sem.at[slot])
 
-    def v_copy(i):
-        slot = lax.rem(i, VALUES)
-        return pltpu.make_async_copy(v_hbm.at[i], vb.at[slot], v_sem.at[slot])
-
-    def last_copy(c):
-        slot, run = (n - 1) % VALUES, pl.ds(ends[c], ends[c + 1] - ends[c])
-        return pltpu.make_async_copy(v_hbm.at[n - 1, run], vb.at[slot, run], last_sem.at[c])
+    def v_copy(i, h):
+        slot, run = lax.rem(i, VALUES), pl.ds(h * half, half)
+        return pltpu.make_async_copy(v_hbm.at[i, run], vb.at[slot, run], v_sem.at[slot, h])
 
     def part_copy(d, first, count, late, slot):
         ref = parts.at[slot, pl.ds(first, count)]
@@ -74,14 +67,10 @@
         stats[me, 0] = jnp.where(lane == i, high, stats[me, 0])
         stats[me, 1] = jnp.where(lane == i, total, stats[me, 1])
 
-    def seen(i, u, begin, end):
-        slot, h = lax.rem(i, VALUES), begin // half
+    def seen(i, u, h):
         w = p_bufs[u].at[lax.rem(lax.div(i, 2), LAG // 2)]
-        w = w[h * heads : (h + 1) * heads, begin - h * half : end - h * half]
-        return jnp.dot(w, vb[slot, begin:end], preferred_element_type=jnp.float32)
-
-    def seen_all(i, u):
-        return seen(i, u, 0, half) + seen(i, u, half, rows)
+        values = vb[lax.rem(i, VALUES), h * half : (h + 1) * half]
+        return jnp.dot(w[h * heads : (h + 1) * heads], values, preferred_element_type=jnp.float32)
 
     def keep(i, o):
         parts[me, i] = o.astype(jnp.bfloat16)
@@ -111,20 +100,16 @@
     for i in range(2):
         k_copy(KEYS + i).start(priority=1)
     for i in range(VALUES - LAG + 2):
-        v_copy(i).start(priority=1)
-
-    def start_last():
-        for c in range(len(CUTS) + 1):
-            last_copy(c).start(priority=1)
+        start_values(i)
+
+    def start_values(i):
+        for h in range(2):
+            v_copy(i, h).start(priority=1)
 
     def next_values(i):
-        @pl.when(i < n - 1)
+        @pl.when(i < n)
         def _():
-            v_copy(i).start(priority=1)
-
-        @pl.when(i == n - 1)
-        def _():
-            start_last()
+            start_values(i)
 
     def early(values, j, carry):
         for u in range(2):
@@ -135,7 +120,7 @@
         for u in range(2):
             k_copy(2 * j + u + KEYS).start(priority=1)
             if values:
-                v_copy(2 * j + u - LAG + VALUES).start(priority=1)
+                start_values(2 * j + u - LAG + VALUES)
         return carry
 
     first = max(1, (LAG - VALUES) // 2)
@@ -146,10 +131,11 @@
     def step(j, carry):
         for u in range(2):
             k_copy(2 * j + u).wait()
-            v_copy(2 * j + u - LAG).wait()
+            for h in range(2):
+                v_copy(2 * j + u - LAG, h).wait()
         for u in range(2):
             t = 2 * j + u
-            keep(t - LAG, seen_all(t - LAG, u))
+            keep(t - LAG, seen(t - LAG, u, 0) + seen(t - LAG, u, 1))
             scores(t, u)
             weights(t - 1, 1 - u)
         share(2 * j - LAG, 2, 0)
@@ -172,24 +158,23 @@
     def late(j, carry):
         for u in range(2):
             i = 2 * j + u
-            v_copy(i).wait()
-            keep(i, seen_all(i, u))
+            for h in range(2):
+                v_copy(i, h).wait()
+            keep(i, seen(i, u, 0) + seen(i, u, 1))
         share(2 * j, 2, 0)
         for u in range(2):
             next_values(2 * j + u + VALUES)
         return carry
 
     lax.fori_loop((n - LAG) // 2, n // 2 - 1, late, 0)
-    v_copy(n - 2).wait()
-    keep(n - 2, seen_all(n - 2, 0))
-    share(n - 2, 1, 1)
-    o = None
-    for c in range(len(CUTS) + 1):
-        last_copy(c).wait()
-        x = seen(n - 1, 1, ends[c], ends[c + 1])
-        o = x if o is None else o + x
-    keep(n - 1, o)
-    share(n - 1, 1, 1)
+    for i in (n - 2, n - 1):
+        o = None
+        for h in range(2):
+            v_copy(i, h).wait()
+            x = seen(i, i % 2, h)
+            o = x if o is None else o + x
+        keep(i, o)
+        share(i, 1, i // (n - 1))
 
     for d in range(1, size):
         stat_copy(d, source(d)).wait_recv()
@@ -204,13 +189,12 @@
         out[i] = functools.reduce(jnp.add, terms).astype(out.dtype)
 
     for d in range(1, size):
-        part_copy(d, 0, n - 2, 0, source(d)).wait_recv()
-    for i in range(n - 2):
+        part_copy(d, 0, n - 1, 0, source(d)).wait_recv()
+    for i in range(n - 1):
         together(i)
     for d in range(1, size):
-        part_copy(d, n - 2, 2, 1, source(d)).wait_recv()
-    for x in range(2):
-        together(n - 2 + x)
+        part_copy(d, n - 1, 1, 1, source(d)).wait_recv()
+    together(n - 1)
     for d in range(1, size):
         stat_copy(d, me).wait_send()
         part_copy(d, 0, n, 0, me).wait_send()
@@ -226,8 +210,19 @@
         half = rows // 2
         f32 = jnp.float32
         dma = pltpu.SemaphoreType.DMA
+
+        def scoped(*refs):
+            pl.run_scoped(
+                functools.partial(kernel, n, key_heads, *refs),
+                dma,
+                dma((KEYS,)),
+                dma((VALUES, 2)),
+                dma((size - 1,)),
+                dma((size - 1,)),
+            )
+
         return pl.pallas_call(
-            functools.partial(kernel, n, (key_heads,)),
+            scoped,
             out_shape=pltpu.VMEM(q.shape, q.dtype),
             in_specs=[pl.BlockSpec(memory_space=pl.ANY)] * 3,
             out_specs=pl.BlockSpec(memory_space=pltpu.VMEM),
@@ -240,13 +235,7 @@
                 *[pltpu.VMEM((heads, 128), f32)] * 2,
                 pltpu.VMEM((size, 2, heads, 128), f32),
                 pltpu.VMEM((size, n, heads, head), jnp.bfloat16),
-                dma,
-                dma((KEYS,)),
-                dma((VALUES,)),
-                dma((len(CUTS) + 1,)),
-                dma((size - 1,)),
                 dma((size - 1, 2)),
-                dma((size - 1,)),
                 dma((size - 1,)),
             ],
             compiler_params=pltpu.CompilerParams(collective_id=0, has_side_effects=True, vmem_limit_bytes=60 * 2**20),

time: 46.3 us -> 46 us (level)
  no operation moved by 1% of the time
where the time goes in v3:
time: 46 us; the launch traced here: 45.9 us
  Pallas kernels  45.3 us (98%)
  local copies, waits for them, and re-layouts  0.68 us (1%)
    pallas_call x1, Pallas kernels, step(): pl.pallas_call(scoped, out_shape=pltpu.VMEM(q.shape, q.dtype), in_specs=[...  45.3 us

profile of v3, /device:TPU:0, one launch (start us, length us, event | category | flops | bytes accessed | tf_op | source)
XLA Modules:
  0.0 45.9 jit_solution(9192388159527265119)
XLA Ops:
  0.0 45.3 %attend.1 = bf16[32,24,128]{2,1,0:T(8,128)(2,1)S(1)} custom-call(bf16[32,24,128]{2,1,0:T(8,128)(2,1)} %refs_0_.1, bf16[32,8192,128]{2,1,0:T(8,128)(2,1)} %bitcast.refs_1_, bf16[32,8192,128]{2,1,0:T(8,128)(2,1)} %bitcast.1.refs_2_), custom_call_target="tpu_custom_call" | custom-call | tf_op jit(solution)/shard_map/attend/pallas_call | solution.py:224
  45.3 0.7 %copy.5 = bf16[32,24,128]{2,1,0:T(8,128)(2,1)} copy(bf16[32,24,128]{2,1,0:T(8,128)(2,1)S(1)} %attend.1) | data formatting | bytes 393216

commit v4 on v3

--- a/solution.py
+++ b/solution.py
@@ -168,11 +168,14 @@
 
     lax.fori_loop((n - LAG) // 2, n // 2 - 1, late, 0)
     for i in (n - 2, n - 1):
-        o = None
-        for h in range(2):
-            v_copy(i, h).wait()
-            x = seen(i, i % 2, h)
-            o = x if o is None else o + x
+        v_copy(i, 0).wait()
+        if i == n - 1:
+            m0[...] = seen(i, i % 2, 0)
+            v_copy(i, 1).wait()
+            o = m0[...] + seen(i, i % 2, 1)
+        else:
+            v_copy(i, 1).wait()
+            o = seen(i, i % 2, 0) + seen(i, i % 2, 1)
         keep(i, o)
         share(i, 1, i // (n - 1))
 

time: 46 us -> 46 us (level)
  no operation moved by 1% of the time
where the time goes in v4:
time: 46 us; the launch traced here: 45.9 us
  Pallas kernels  45.2 us (98%)
  local copies, waits for them, and re-layouts  0.68 us (1%)
    pallas_call x1, Pallas kernels, step(): pl.pallas_call(scoped, out_shape=pltpu.VMEM(q.shape, q.dtype), in_specs=[...  45.2 us

profile of v4, /device:TPU:0, one launch (start us, length us, event | category | flops | bytes accessed | tf_op | source)
XLA Modules:
  0.0 45.9 jit_solution(5114303954312811188)
XLA Ops:
  0.0 45.2 %attend.1 = bf16[32,24,128]{2,1,0:T(8,128)(2,1)S(1)} custom-call(bf16[32,24,128]{2,1,0:T(8,128)(2,1)} %refs_0_.1, bf16[32,8192,128]{2,1,0:T(8,128)(2,1)} %bitcast.refs_1_, bf16[32,8192,128]{2,1,0:T(8,128)(2,1)} %bitcast.1.refs_2_), custom_call_target="tpu_custom_call" | custom-call | tf_op jit(solution)/shard_map/attend/pallas_call | solution.py:227
  45.2 0.7 %copy.5 = bf16[32,24,128]{2,1,0:T(8,128)(2,1)} copy(bf16[32,24,128]{2,1,0:T(8,128)(2,1)S(1)} %attend.1) | data formatting | bytes 393216
